TPU v7x, 32 devices: a whole 2x2x4 slice. The times are simulated.
32 devices in a mesh: root: 4 (over z), virt: 4 (over y, x), occ: 2 (over core).
Axes of the slice: x: 2, y: 2, z: 4, core: 2. Of those that a mesh axis runs over, the one named last changes fastest.
Arguments:
- trial_singles: bfloat16 [8, 96], P('root'), may hold values from -6 to 6
- trial_doubles: bfloat16 [8, 480, 9216], P('root', 'virt', 'occ'), may hold values from -6 to 6
- occ_fock: bfloat16 [96, 96], replicated, may hold values from -0.625 to 0.625
- virt_fock: bfloat16 [480, 480], replicated, may hold values from -0.25 to 0.25
- w_ovoo: bfloat16 [96, 480, 9216], P('occ', 'virt', 'root'), may hold values from -0.625 to 0.625
- w_ooov: bfloat16 [96, 480, 9216], P('occ', 'virt', 'root'), may hold values from -0.0029296875 to 0.0029296875
- converged: int32 [8], replicated, may hold values from 0 to 1, as said below
Outputs:
- sigma_doubles: bfloat16 [8, 480, 9216], P('root', 'virt', 'occ')
- sigma_singles: float32 [8, 96], P('root')
- subspace: float32 [8, 8], P('root')
Inputs may be any that keep to these rules, and one draw needn't show every extreme that they name: `converged`: exactly 4 roots are active (0). In every draw at least one aligned block of 2 roots has all its roots active; other blocks may have none.
All inputs are finite; a program needn't handle non-finite values.
Results may differ from a plain program's by a relative error of at most 0.0044.
Values may be sent and summed in bfloat16 or wider, within the bound.
A program may use at most 256 MiB of HBM per device.

v0:
```python
import math

import jax
import jax.numpy as jnp
from jax import lax
from jax.sharding import PartitionSpec as P


def flat_pairs(left, right):
    return lax.dot_general(
        left.reshape(left.shape[0], -1),
        right.reshape(right.shape[0], -1),
        (((1,), (1,)), ((), ())),
        preferred_element_type=jnp.float32,
    )


def local(trial_singles, trial_doubles, occ_fock, virt_fock, w_ovoo, w_ooov, converged):
    local_roots, virt_local, pair_local = trial_doubles.shape
    occ_count = occ_fock.shape[0]
    virt_count = virt_fock.shape[0]
    root_count = converged.shape[0]
    root_groups = lax.axis_size("root")
    occ_groups = lax.axis_size("occ")
    root_index = lax.axis_index("root")
    occ_index = lax.axis_index("occ")
    occ_half = occ_count // occ_groups
    block_pairs = occ_count * occ_count // root_groups
    own_start = occ_index * occ_half
    active = (1 - converged).astype(jnp.float32)
    own_active = lax.dynamic_slice_in_dim(active, root_index * local_roots, local_roots)
    singles_all = lax.all_gather(trial_singles, "root", axis=0, tiled=True)
    gathered = lax.all_gather(trial_doubles, "occ", axis=2, tiled=True)
    fock_cols = lax.dynamic_slice_in_dim(occ_fock, own_start, occ_half, 1)
    batch_rows = local_roots * virt_local
    stacked = gathered.reshape(batch_rows, occ_count, occ_count)
    first_term = jnp.einsum(
        "ki,bkj->bij", fock_cols, stacked, preferred_element_type=jnp.float32
    ).reshape(local_roots, virt_local, pair_local)
    own_rows = trial_doubles.reshape(batch_rows, occ_half, occ_count)
    second_term = jnp.einsum(
        "bik,kj->bij", own_rows, occ_fock, preferred_element_type=jnp.float32
    ).reshape(local_roots, virt_local, pair_local)
    doubles_block = lax.all_to_all(gathered, "root", split_axis=2, concat_axis=0, tiled=True)
    partial_coupling = flat_pairs(doubles_block, w_ooov)
    coupling_part = lax.dynamic_update_slice(
        jnp.zeros((root_count, occ_count), jnp.float32), partial_coupling, (jnp.int32(0), own_start)
    )
    coupling = lax.psum(coupling_part, ("root", "virt", "occ"))
    singles_fock = jnp.dot(singles_all, occ_fock, preferred_element_type=jnp.float32)
    singles_every = active[:, None] * (-singles_fock - 0.5 * coupling)
    sigma_singles = lax.dynamic_slice_in_dim(singles_every, root_index * local_roots, local_roots)
    singles_cols = lax.dynamic_slice_in_dim(singles_all, own_start, occ_half, 1)
    outer_part = (
        -jnp.dot(singles_cols, w_ovoo.reshape(occ_half, -1), preferred_element_type=jnp.float32)
    ).reshape(root_count, virt_local, block_pairs)
    product = jnp.einsum(
        "ac,ncp->nap",
        virt_fock,
        lax.all_to_all(trial_doubles, "virt", split_axis=2, concat_axis=1, tiled=True),
        preferred_element_type=jnp.float32,
    ).astype(jnp.bfloat16)
    vv_term = lax.all_to_all(product, "virt", split_axis=1, concat_axis=2, tiled=True)
    vv_value = vv_term.astype(jnp.float32)
    outer_own = lax.all_to_all(outer_part, "root", split_axis=0, concat_axis=2, tiled=True)
    outer_half = lax.psum_scatter(outer_own, "occ", scatter_dimension=2, tiled=True)
    summed = vv_value + outer_half - first_term - second_term
    sigma_doubles = (own_active[:, None, None] * summed).astype(jnp.bfloat16)
    trial_piece, sigma_piece = (
        lax.all_to_all(trial_doubles, "root", split_axis=2, concat_axis=0, tiled=True),
        lax.all_to_all(sigma_doubles, "root", split_axis=2, concat_axis=0, tiled=True),
    )
    doubles_part = lax.psum(flat_pairs(trial_piece, sigma_piece), ("root", "virt", "occ"))
    singles_part = jnp.dot(
        singles_all.astype(jnp.float32), singles_every.T, precision=lax.Precision.HIGHEST
    )
    whole_matrix = doubles_part / math.sqrt(
        occ_count * occ_count * virt_count
    ) + singles_part / math.sqrt(occ_count)
    subspace = lax.dynamic_slice_in_dim(whole_matrix, root_index * local_roots, local_roots, 0)
    return (sigma_doubles, sigma_singles, subspace)


def solution(mesh):
    placed = (
        P("root", None),
        P("root", "virt", "occ"),
        P(),
        P(),
        P("occ", "virt", "root"),
        P("occ", "virt", "root"),
        P(),
    )
    return jax.shard_map(
        local,
        mesh=mesh,
        in_specs=placed,
        out_specs=(P("root", "virt", "occ"), P("root", None), P("root", None)),
        check_vma=False,
    )
```

profile of v0, /device:TPU:0, one launch (start us, length us, event | category | flops | bytes accessed | tf_op | source)
XLA Modules:
  0.0 595.7 jit_solution(10986336026013833331)
XLA Ops:
  7.2 6.9 %copy.53 = bf16[2,120,4608]{1,0,2:T(2,128)(2,1)} copy(bf16[2,120,4608]{2,1,0:T(8,128)(2,1)} %param.8) | data formatting | bytes 4423680 | tf_op args[1]
  14.1 5.2 all-to-all-start
  19.3 24.4 %copy.79 = bf16[6,8,120,2304]{3,1,2,0:T(8,128)(2,1)} copy(bf16[6,8,120,2304]{3,2,1,0:T(8,128)(2,1)} %bitcast.88) | data formatting | bytes 53084160
  43.7 11.1 %all-gather = bf16[4,2,96]{2,1,0:T(2,128)(2,1)S(1)} all-gather(bf16[1,2,96]{2,1,0:T(2,128)(2,1)S(1)} %bitcast.102), channel_id=1, replica_groups=mesh['root'=4,'virt'=4,'occ'=2] {'root'}, dimensions={0}, use_global_device_ids=true | all-gather | bytes 1920 | tf_op jit(solution)/shard_map/all_gather | solution.py:32
  54.8 10.4 %convolution_negate_fusion = f32[8,276480]{1,0:T(8,128)S(1)} fusion(bf16[48,276480]{1,0:T(8,128)(2,1)} %bitcast.84, bf16[8,96]{1,0:T(8,128)(2,1)S(1)} %bitcast.99, s32[]{:T(128)S(6)} %select_n.5), kind=kOutput, calls=%fused_computation | convolution fusion | flops 214548480 | bytes 35390980 | tf_op jit(solution)/shard_map/dot_general | solution.py:55
  65.3 6.1 %copy.57 = f32[8,120,2304]{2,1,0:T(8,128)} copy(f32[8,120,2304]{2,0,1:T(8,128)S(1)} %bitcast.85) | data formatting | bytes 17694720 | tf_op jit(solution)/shard_map/reshape | solution.py:56
  71.4 5.7 all-to-all-start.2
  77.8 4.4 copy.54
  88.3 180.0 %all-to-all-done.2 = f32[8,120,2304]{2,1,0:T(8,128)} async-done(((f32[8,120,2304]{2,1,0:T(8,128)}), f32[8,120,2304]{2,1,0:T(8,128)}, u32[]{:S(2)}, u32[]{:S(2)}) %all-to-all-start.2) | async-done | bytes 8847392 | tf_op jit(solution)/shard_map/all_to_all | solution.py:65
  272.1 14.5 %copy.58 = f32[2,120,4,2304]{1,0,3,2:T(2,128)} copy(f32[2,120,4,2304]{3,1,0,2:T(8,128)} %bitcast.12) | data formatting | bytes 17694720 | tf_op jit(solution)/shard_map/all_to_all | solution.py:65
  286.6 10.8 %all-to-all-done.1 = bf16[2,480,1152]{2,0,1:T(2,128)(2,1)S(1)} async-done(((bf16[2,480,1152]{2,0,1:T(2,128)(2,1)}), bf16[2,480,1152]{2,0,1:T(2,128)(2,1)S(1)}, u32[]{:S(2)}, u32[]{:S(2)}) %all-to-all-start.1) | async-done | bytes 2211872 | tf_op jit(solution)/shard_map/all_to_all | solution.py:63
  302.6 12.7 %copy.65 = bf16[2,120,9216]{1,0,2:T(2,128)(2,1)} copy(bf16[2,120,9216]{2,1,0:T(8,128)(2,1)} %all-gather.3.cloned.1.call-done) | data formatting | bytes 8847360 | tf_op jit(solution)/shard_map/all_gather | solution.py:33
  315.3 40.6 %all-to-all-done.5 = bf16[2,120,4608]{1,0,2:T(2,128)(2,1)S(1)} async-done(((bf16[2,120,4608]{1,0,2:T(2,128)(2,1)}), bf16[2,120,4608]{1,0,2:T(2,128)(2,1)S(1)}, u32[]{:S(2)}, u32[]{:S(2)}) %all-to-all-start.5) | async-done | bytes 2211872 | tf_op jit(solution)/shard_map/all_to_all | solution.py:70
  356.0 5.1 all-to-all-start.3
  361.1 5.9 reshape.49
  367.0 4.7 fusion.11
  371.6 7.1 %reshape.50 = f32[2,120,4608]{1,0,2:T(2,128)} reshape(f32[240,48,96]{0,2,1:T(8,128)} %fusion.11) | data formatting | bytes 8847360 | tf_op jit(solution)/shard_map/reshape | solution.py:43
  380.1 8.9 %copy.56 = f32[2,4,120,1152]{2,0,3,1:T(2,128)} copy(bf16[2,4,120,1152]{3,0,2,1:T(2,128)(2,1)} %bitcast.95) | data formatting | bytes 6635520 | tf_op jit(solution)/shard_map/convert_element_type | solution.py:64
  389.0 9.5 %reshape.62 = bf16[240,96,96]{2,1,0:T(8,128)(2,1)} reshape(bf16[2,120,9216]{2,1,0:T(8,128)(2,1)} %all-gather.3.cloned.1.call-done) | data formatting | bytes 8847360 | tf_op jit(solution)/shard_map/reshape | solution.py:36
  398.6 9.2 %copy.61 = bf16[240,96,96]{0,1,2:T(8,128)(2,1)} copy(bf16[240,96,96]{2,1,0:T(8,128)(2,1)} %reshape.62) | data formatting | bytes 8847360 | tf_op jit(solution)/shard_map/reshape | solution.py:36
  411.0 4.8 copy.62
  415.9 7.1 %reshape.48 = f32[2,120,4608]{1,0,2:T(2,128)} reshape(f32[240,48,96]{0,2,1:T(8,128)} %copy.62) | data formatting | bytes 8847360 | tf_op jit(solution)/shard_map/reshape | solution.py:39
  423.0 10.2 %fusion.3 = bf16[2,120,4608]{1,0,2:T(2,128)(2,1)} fusion(f32[2,120,4608]{1,0,2:T(2,128)} %reshape.50, f32[2,120,4608]{1,0,2:T(2,128)} %reshape.48, f32[2,120,9216]{1,0,2:T(2,128)} %all-reduce.4.cloned.1.call-done, u32[]{:T(128)S(6)} %multiply.4, f32[2,4,120,1152]{2,0,3,1:T(2,128)} %copy.56, f32[2]{0:T(128)S(1)} %dynamic_slice.15), kind=kLoop, calls=%fused_computation.5 | loop fusion | flops 5529600 | bytes 19906572 | tf_op jit(solution)/shard_map/convert_element_type | solution.py:68
  433.2 31.7 %all-to-all-done.3 = bf16[2,120,9216]{1,0,2:T(2,128)(2,1)} async-done(((bf16[2,120,9216]{1,0,2:T(2,128)(2,1)}), bf16[2,120,9216]{1,0,2:T(2,128)(2,1)}, u32[]{:S(2)}, u32[]{:S(2)}) %all-to-all-start.3) | async-done | bytes 4423712 | tf_op jit(solution)/shard_map/all_to_all | solution.py:44
  464.9 4.7 all-to-all-start.4
  469.6 24.4 %copy.81 = bf16[6,8,120,2304]{3,1,2,0:T(8,128)(2,1)} copy(bf16[6,8,120,2304]{3,2,1,0:T(8,128)(2,1)} %bitcast.89) | data formatting | bytes 53084160
  500.2 12.3 %copy.66 = bf16[2,120,4,2304]{3,1,0,2:T(8,128)(2,1)} copy(bf16[2,120,4,2304]{1,0,3,2:T(2,128)(2,1)} %bitcast.17) | data formatting | bytes 8847360 | tf_op jit(solution)/shard_map/all_to_all | solution.py:44
  512.5 5.2 copy.80
  517.7 13.4 %fusion.17 = f32[8,48]{1,0:T(8,128)S(1)} fusion(bf16[8,276480]{1,0:T(8,128)(2,1)} %bitcast.87, bf16[48,276480]{1,0:T(8,128)(2,1)} %bitcast.83), kind=kOutput, calls=%fused_computation.27 | convolution fusion | flops 212336640 | bytes 30967296 | tf_op jit(solution)/shard_map/dot_general | solution.py:10
  531.2 6.7 %copy.71 = bf16[2,120,4608]{2,1,0:T(8,128)(2,1)} copy(bf16[2,120,4608]{1,0,2:T(2,128)(2,1)} %fusion.3) | data formatting | bytes 4423680
  537.9 6.8 %copy.67 = bf16[2,120,4,1152]{3,1,0,2:T(8,128)(2,1)} copy(bf16[2,120,4,1152]{1,0,3,2:T(2,128)(2,1)} %bitcast.19) | data formatting | bytes 4423680 | tf_op jit(solution)/shard_map/all_to_all | solution.py:71
  547.8 39.5 %all-reduce.1 = (f32[8,96]{1,0:T(8,128)S(1)}, f32[8,8]{0,1:T(8,128)S(1)}) all-reduce(f32[8,96]{1,0:T(8,128)S(1)} %dynamic_update_slice.3, f32[8,8]{0,1:T(8,128)S(1)} %convolution_bitcast_fusion.1), channel_id=1, replica_groups=mesh['root'=4,'virt'=4,'occ'=2] {'root','virt','occ'}, use_global_device_ids=true, to_apply=%region_1.0 | all-reduce | flops 832 | bytes 6656 | tf_op jit(solution)/shard_map/psum | solution.py:49
  (41 shorter events, 30.6 us)
Async XLA Ops:
  7.2 75.1 %copy-start = (bf16[480,480]{1,0:T(8,128)(2,1)S(1)}, bf16[480,480]{1,0:T(8,128)(2,1)}, u32[]{:S(2)}) copy-start(bf16[480,480]{1,0:T(8,128)(2,1)} %param.10) | copy-start | bytes 1382404
  14.1 57.3 %all-to-all-start = ((bf16[2,120,4608]{1,0,2:T(2,128)(2,1)}), bf16[2,120,4608]{1,0,2:T(2,128)(2,1)S(1)}, u32[]{:S(2)}, u32[]{:S(2)}) async-start(bf16[2,120,4608]{1,0,2:T(2,128)(2,1)} %copy.53), calls=%async_computation | async-start | bytes 4718592 | tf_op jit(solution)/shard_map/all_to_all | solution.py:60
  19.3 24.4 %copy-start.4 = (bf16[2,96]{1,0:T(2,128)(2,1)S(1)}, bf16[2,96]{1,0:T(2,128)(2,1)}, u32[]{:S(2)}) copy-start(bf16[2,96]{1,0:T(2,128)(2,1)} %param.7) | copy-start | bytes 1156
  71.4 196.8 %all-to-all-start.2 = ((f32[8,120,2304]{2,1,0:T(8,128)}), f32[8,120,2304]{2,1,0:T(8,128)}, u32[]{:S(2)}, u32[]{:S(2)}) async-start(f32[8,120,2304]{2,1,0:T(8,128)} %copy.57), calls=%async_computation.2 | async-start | bytes 17694720 | tf_op jit(solution)/shard_map/all_to_all | solution.py:65
  77.1 225.4 %all-gather.3.cloned.1.call-start = ((), (), s32[]{:S(2)}) async-start(), calls=%async_computation.6 | async-start | bytes 6635520 | tf_op jit(solution)/shard_map/all_gather | solution.py:33
  268.2 29.2 %all-to-all-start.1 = ((bf16[2,480,1152]{2,0,1:T(2,128)(2,1)}), bf16[2,480,1152]{2,0,1:T(2,128)(2,1)S(1)}, u32[]{:S(2)}, u32[]{:S(2)}) async-start(bf16[2,480,1152]{2,0,1:T(2,128)(2,1)} %copy.55), calls=%async_computation.1 | async-start | bytes 4423680 | tf_op jit(solution)/shard_map/all_to_all | solution.py:63
  272.1 150.9 %all-reduce.4.cloned.1.call-start = ((), (), s32[]{:S(2)}) async-start(), calls=%async_computation.7 | async-start | bytes 18874368
  297.5 1.4 copy-start.2
  298.8 57.1 %all-to-all-start.5 = ((bf16[2,120,4608]{1,0,2:T(2,128)(2,1)}), bf16[2,120,4608]{1,0,2:T(2,128)(2,1)S(1)}, u32[]{:S(2)}, u32[]{:S(2)}) async-start(bf16[2,120,4608]{1,0,2:T(2,128)(2,1)} %copy.53), calls=%async_computation.5 | async-start | bytes 4718592 | tf_op jit(solution)/shard_map/all_to_all | solution.py:70
  356.0 108.9 %all-to-all-start.3 = ((bf16[2,120,9216]{1,0,2:T(2,128)(2,1)}), bf16[2,120,9216]{1,0,2:T(2,128)(2,1)}, u32[]{:S(2)}, u32[]{:S(2)}) async-start(bf16[2,120,9216]{1,0,2:T(2,128)(2,1)} %copy.65), calls=%async_computation.3 | async-start | bytes 9437184 | tf_op jit(solution)/shard_map/all_to_all | solution.py:44
  361.1 5.9 copy-start.3
  371.6 7.2 %copy-start.5 = (s32[8]{0:T(128)S(1)}, s32[8]{0:T(128)}, u32[]{:S(2)}) copy-start(s32[8]{0:T(128)} %param.13) | copy-start | bytes 100
  371.6 7.2 %copy-start.6 = (u32[32]{0:T(128)S(1)}, u32[32]{0:T(128)}, u32[]{:S(2)}) copy-start(u32[32]{0:T(128)} %constant.35) | copy-start | bytes 388
  464.9 73.0 %all-to-all-start.4 = ((bf16[2,120,4608]{1,0,2:T(2,128)(2,1)}), bf16[2,120,4608]{1,0,2:T(2,128)(2,1)}, u32[]{:S(2)}, u32[]{:S(2)}) async-start(bf16[2,120,4608]{1,0,2:T(2,128)(2,1)} %fusion.3), calls=%async_computation.4 | async-start | bytes 4718592 | tf_op jit(solution)/shard_map/all_to_all | solution.py:71
  537.9 51.0 %copy-start.1 = (bf16[480,480]{1,0:T(8,128)(2,1)S(1)}, bf16[480,480]{1,0:T(8,128)(2,1)}, u32[]{:S(2)}) copy-start(bf16[480,480]{1,0:T(8,128)(2,1)} %param.10) | copy-start | bytes 1382404
Sparse Core Ops, SparseCore 0:
  79.5 15.8 all-gather.2
  286.7 40.7 all-reduce.3
where the time goes:
time: 599 us; the launch traced here: 596 us
  waiting for transfers between devices  264 us (44%)
  local copies, waits for them, and re-layouts  192 us (32%)
  blocking collectives  50.7 us (8%)
  matrix products  36.1 us (6%)
  starting transfers between devices  28.3 us (5%)
  between operations  14.8 us (2%)
  other arithmetic  10.2 us (2%)
    all_to_all x1, waiting for transfers between devices, local(): lax.all_to_all(outer_part, 'root', split_axis=0, concat_axis=2, tiled=True)  180 us
    unnamed x23, local copies, waits for them, and re-layouts  74 us
    all_to_all x1, waiting for transfers between devices, local(): lax.all_to_all(trial_doubles, 'root', split_axis=2, concat_axis=0, tiled=...  40.6 us
    psum x1, blocking collectives, local(): coupling = lax.psum(coupling_part, ('root', 'virt', 'occ'))  39.5 us
    all_to_all x1, waiting for transfers between devices, local(): lax.all_to_all(gathered, 'root', split_axis=2, concat_axis=0, tiled=True)  31.7 us
    reshape x2, local copies, waits for them, and re-layouts, local(): stacked = gathered.reshape(batch_rows, occ_count, occ_count)  18.8 us
    dot_general x2, matrix products, flat_pairs(): lax.dot_general(left.reshape(left.shape[0], -1), right.reshape(right.shap...  14.6 us
    all_to_all x1, local copies, waits for them, and re-layouts, local(): lax.all_to_all(outer_part, 'root', split_axis=0, concat_axis=2, tiled=True)  14.5 us
  transfers between devices with their start and end apart: 8, of which 4 were waited for; matrix products, arithmetic and copies ran while one was open for 37% of the time, Pallas kernels for 0%

commit v1 on v0

--- a/solution.py
+++ b/solution.py
@@ -3,6 +3,8 @@
 import jax
 import jax.numpy as jnp
 from jax import lax
+from jax.experimental import pallas as pl
+from jax.experimental.pallas import tpu as pltpu
 from jax.sharding import PartitionSpec as P
 
 
@@ -15,7 +17,7 @@
     )
 
 
-def local(trial_singles, trial_doubles, occ_fock, virt_fock, w_ovoo, w_ooov, converged):
+def plain(trial_singles, trial_doubles, occ_fock, virt_fock, w_ovoo, w_ooov, converged):
     local_roots, virt_local, pair_local = trial_doubles.shape
     occ_count = occ_fock.shape[0]
     virt_count = virt_fock.shape[0]
@@ -81,6 +83,383 @@
     return (sigma_doubles, sigma_singles, subspace)
 
 
+ROWS = 8
+
+
+def call(body, grid, ins, outs, shapes, scratch=(), flops=0, moved=0, semantics=None):
+    return pl.pallas_call(
+        body,
+        grid=grid,
+        in_specs=ins,
+        out_specs=outs,
+        out_shape=shapes,
+        scratch_shapes=list(scratch),
+        compiler_params=pltpu.CompilerParams(
+            dimension_semantics=("arbitrary",) * len(grid), vmem_limit_bytes=48 * 1024 * 1024
+        ),
+        cost_estimate=pl.CostEstimate(flops=flops, bytes_accessed=moved, transcendentals=0),
+    )
+
+
+SCALAR = pl.BlockSpec(memory_space=pltpu.SMEM)
+
+
+def rows_flat(block):
+    count, rows, width = block.shape
+    return block.astype(jnp.float32).reshape(count * rows, width).astype(jnp.bfloat16)
+
+
+def outer_body(core, mix, weights, kept, sent):
+    roots, rows, width = kept.shape
+    value = jnp.dot(mix[...], rows_flat(weights[...]), preferred_element_type=jnp.float32)
+    value = value.reshape(roots, rows, 2 * width)
+    low, high = value[:, :, :width], value[:, :, width:]
+    first = core[0] == 0
+    kept[...] = jnp.where(first, low, high)
+    sent[...] = jnp.where(first, high, low).astype(jnp.bfloat16)
+
+
+def outer_terms(core, singles_cols, weights):
+    count, virt_local, pairs = weights.shape
+    roots = singles_cols.shape[0]
+    width = pairs // 2
+    eye = jnp.eye(ROWS, dtype=jnp.bfloat16)
+    mix = (-singles_cols[:, None, :, None] * eye[None, :, None, :]).reshape(
+        roots * ROWS, count * ROWS
+    )
+    piece = pl.BlockSpec((roots, ROWS, width), lambda a: (0, a, 0))
+    return call(
+        outer_body,
+        (virt_local // ROWS,),
+        [
+            SCALAR,
+            pl.BlockSpec(mix.shape, lambda a: (0, 0)),
+            pl.BlockSpec((count, ROWS, pairs), lambda a: (0, a, 0)),
+        ],
+        [piece, piece],
+        [
+            jax.ShapeDtypeStruct((roots, virt_local, width), jnp.float32),
+            jax.ShapeDtypeStruct((roots, virt_local, width), jnp.bfloat16),
+        ],
+        flops=2 * roots * ROWS * weights.size,
+        moved=2 * weights.size,
+    )(core, mix, weights)
+
+
+def coupling_body(core, own, other, weights, total, held):
+    width = own.shape[2]
+
+    @pl.when(pl.program_id(0) == 0)
+    def _():
+        held[...] = jnp.zeros_like(held)
+
+    here = pl.multiple_of(core[0] * width, 128)
+    there = pl.multiple_of((1 - core[0]) * width, 128)
+    dims = (((1,), (1,)), ((), ()))
+    held[...] += lax.dot_general(
+        rows_flat(own[...]), rows_flat(weights[:, :, pl.ds(here, width)]), dims,
+        preferred_element_type=jnp.float32,
+    ) + lax.dot_general(
+        rows_flat(other[...]), rows_flat(weights[:, :, pl.ds(there, width)]), dims,
+        preferred_element_type=jnp.float32,
+    )
+
+    @pl.when(pl.program_id(0) == pl.num_programs(0) - 1)
+    def _():
+        total[...] = held[...]
+
+
+def same_row(table, left, rows, right):
+    eye = jnp.eye(rows, dtype=jnp.float32)
+    return jnp.sum(table.reshape(left, rows, right, rows) * eye[None, :, None, :], axis=(1, 3))
+
+
+def coupling_sums(core, own, other, weights):
+    count, virt_local, pairs = weights.shape
+    roots, _, width = own.shape
+    shape = (roots * ROWS, count * ROWS)
+    piece = pl.BlockSpec((roots, ROWS, width), lambda a: (0, a, 0))
+    table = call(
+        coupling_body,
+        (virt_local // ROWS,),
+        [SCALAR, piece, piece, pl.BlockSpec((count, ROWS, pairs), lambda a: (0, a, 0))],
+        pl.BlockSpec(shape, lambda a: (0, 0)),
+        jax.ShapeDtypeStruct(shape, jnp.float32),
+        [pltpu.VMEM(shape, jnp.float32)],
+        flops=2 * roots * ROWS * weights.size,
+        moved=2 * weights.size,
+    )(core, own, other, weights)
+    return same_row(table, roots, ROWS, count)
+
+
+def project_body(left, right, total, held):
+    @pl.when(pl.program_id(0) == 0)
+    def _():
+        held[...] = jnp.zeros_like(held)
+
+    held[...] += lax.dot_general(
+        rows_flat(left[...]), rows_flat(right[...]), (((1,), (1,)), ((), ())),
+        preferred_element_type=jnp.float32,
+    )
+
+    @pl.when(pl.program_id(0) == pl.num_programs(0) - 1)
+    def _():
+        total[...] = held[...]
+
+
+def project(left, right):
+    roots, virt_local, width = left.shape
+    rows = next(n for n in (40, 24, 16, 8) if virt_local % n == 0)
+    shape = (roots * rows, roots * rows)
+    piece = pl.BlockSpec((roots, rows, width), lambda a: (0, a, 0))
+    table = call(
+        project_body,
+        (virt_local // rows,),
+        [piece, piece],
+        pl.BlockSpec(shape, lambda a: (0, 0)),
+        jax.ShapeDtypeStruct(shape, jnp.float32),
+        [pltpu.VMEM(shape, jnp.float32)],
+        flops=2 * roots * rows * left.size,
+        moved=4 * left.size,
+    )(left, right)
+    return same_row(table, roots, rows, roots)
+
+
+def occ_body(tile, count, own, other, own_fock, other_fock, unit, second, out):
+    column = pl.program_id(0)
+
+    def spread(rows):
+        parts = [unit[...] * rows[k : k + 1, :] for k in range(rows.shape[0])]
+        return jnp.concatenate(parts, axis=0).astype(jnp.bfloat16)
+
+    def step(k, total):
+        cut = pl.ds(pl.multiple_of(k * tile, 128), tile)
+        total = total + jnp.dot(
+            own[:, cut], spread(own_fock[k]), preferred_element_type=jnp.float32
+        )
+        return total + jnp.dot(
+            other[:, cut], spread(other_fock[k]), preferred_element_type=jnp.float32
+        )
+
+    here = pl.ds(pl.multiple_of(column * tile, 128), tile)
+    begin = jnp.dot(own[:, here], second[...], preferred_element_type=jnp.float32)
+    out[...] = lax.fori_loop(0, count, step, begin)
+
+
+def occ_terms(own, other, fock_own, fock_other, occ_fock):
+    rows, pairs = own.shape
+    occ_count = occ_fock.shape[0]
+    group = 128 // math.gcd(occ_count, 128)
+    tile = group * occ_count
+    count = pairs // tile
+    eye = jnp.eye(occ_count, dtype=jnp.float32)
+    unit = jnp.tile(eye, (1, group))
+    second = (
+        jnp.eye(group, dtype=jnp.bfloat16)[:, None, :, None] * occ_fock[None, :, None, :]
+    ).reshape(tile, tile)
+
+    def wide(block):
+        return jnp.repeat(block.astype(jnp.float32), occ_count, axis=1).reshape(count, group, pairs)
+
+    whole = pl.BlockSpec((rows, pairs), lambda c: (0, 0))
+    fock_spec = pl.BlockSpec((count, group, tile), lambda c: (0, 0, c))
+
+    def body(*refs):
+        occ_body(tile, count, *refs)
+
+    return call(
+        body,
+        (count,),
+        [
+            whole,
+            whole,
+            fock_spec,
+            fock_spec,
+            pl.BlockSpec(unit.shape, lambda c: (0, 0)),
+            pl.BlockSpec(second.shape, lambda c: (0, 0)),
+        ],
+        pl.BlockSpec((rows, tile), lambda c: (0, c)),
+        jax.ShapeDtypeStruct((rows, pairs), jnp.float32),
+        flops=4 * rows * pairs * pairs,
+        moved=8 * rows * pairs,
+    )(own, other, wide(fock_own), wide(fock_other), unit, second)
+
+
+def virt_body(fock, amps, out):
+    blocks = amps.shape[0]
+    for b in range(blocks):
+        total = jnp.dot(fock[b, 0], amps[0, 0], preferred_element_type=jnp.float32)
+        for c in range(1, blocks):
+            total += jnp.dot(fock[b, c], amps[c, 0], preferred_element_type=jnp.float32)
+        out[b, 0] = total.astype(jnp.bfloat16)
+
+
+def virt_product(virt_fock, amps):
+    blocks, roots, virt_local, width = amps.shape
+    fock = virt_fock.reshape(blocks, virt_local, blocks, virt_local).transpose(0, 2, 1, 3)
+    piece = pl.BlockSpec((blocks, 1, virt_local, width), lambda n: (0, n, 0, 0))
+    return call(
+        virt_body,
+        (roots,),
+        [pl.BlockSpec(fock.shape, lambda n: (0, 0, 0, 0)), piece],
+        piece,
+        jax.ShapeDtypeStruct(amps.shape, jnp.bfloat16),
+        flops=2 * blocks * virt_local * amps.size,
+        moved=4 * amps.size,
+    )(fock, amps)
+
+
+def sigma_body(core, active, vv, mine, theirs, occ_sum, sigma, kept, sent):
+    width = mine.shape[3]
+    first = core[0] == 0
+    weight = active[pl.program_id(0)]
+    here = mine[0, 0].astype(jnp.float32)
+    there = theirs[0, 0].astype(jnp.float32)
+    low = vv[0, 0].astype(jnp.float32) + jnp.where(first, here, there) - occ_sum[0, :, :width]
+    high = vv[1, 0].astype(jnp.float32) + jnp.where(first, there, here) - occ_sum[0, :, width:]
+    low = weight * low
+    high = weight * high
+    sigma[0, :, :width] = low.astype(jnp.bfloat16)
+    sigma[0, :, width:] = high.astype(jnp.bfloat16)
+    kept[0, 0] = jnp.where(first, low, high).astype(jnp.bfloat16)
+    sent[0, 0] = jnp.where(first, high, low).astype(jnp.bfloat16)
+
+
+def sigma_terms(core, active, vv, mine, theirs, occ_sum):
+    quarters, roots, virt_local, width = mine.shape
+    piece = pl.BlockSpec((1, 1, virt_local, width), lambda n, q: (q, n, 0, 0))
+    full = pl.BlockSpec((1, virt_local, 2 * width), lambda n, q: (n, 0, q))
+    return call(
+        sigma_body,
+        (roots, quarters),
+        [
+            SCALAR,
+            SCALAR,
+            pl.BlockSpec((2, 1, virt_local, width), lambda n, q: (q, n, 0, 0)),
+            piece,
+            piece,
+            full,
+        ],
+        [full, piece, piece],
+        [
+            jax.ShapeDtypeStruct(occ_sum.shape, jnp.bfloat16),
+            jax.ShapeDtypeStruct(mine.shape, jnp.bfloat16),
+            jax.ShapeDtypeStruct(mine.shape, jnp.bfloat16),
+        ],
+        flops=8 * occ_sum.size,
+        moved=14 * occ_sum.size,
+    )(core, active, vv, mine, theirs, occ_sum)
+
+
+def tiled(trial_doubles, virt_fock, occ_fock):
+    _, virt_local, pair_local = trial_doubles.shape
+    occ_count = occ_fock.shape[0]
+    root_groups = lax.axis_size("root")
+    sub = occ_count * occ_count // root_groups // 2
+    tile = occ_count * 128 // math.gcd(occ_count, 128)
+    return (
+        lax.axis_size("occ") == 2
+        and root_groups % 2 == 0
+        and virt_local % ROWS == 0
+        and sub % 128 == 0
+        and sub * lax.axis_size("virt") == pair_local
+        and pair_local % tile == 0
+    )
+
+
+def local(trial_singles, trial_doubles, occ_fock, virt_fock, w_ovoo, w_ooov, converged):
+    if not tiled(trial_doubles, virt_fock, occ_fock):
+        return plain(trial_singles, trial_doubles, occ_fock, virt_fock, w_ovoo, w_ooov, converged)
+    local_roots, virt_local, pair_local = trial_doubles.shape
+    occ_count = occ_fock.shape[0]
+    virt_count = virt_fock.shape[0]
+    root_count = converged.shape[0]
+    root_groups = lax.axis_size("root")
+    virt_groups = lax.axis_size("virt")
+    root_index = lax.axis_index("root")
+    occ_index = lax.axis_index("occ")
+    occ_half = occ_count // 2
+    quarters = root_groups // 2
+    sub = pair_local // quarters // 2
+    own_start = occ_index * occ_half
+    other_start = (1 - occ_index) * occ_half
+    core = occ_index.astype(jnp.int32).reshape(1)
+    first_core = occ_index == 0
+    active = (1 - converged).astype(jnp.float32)
+    own_active = lax.dynamic_slice_in_dim(active, root_index * local_roots, local_roots)
+
+    def swap(value):
+        return lax.ppermute(value, "occ", [(0, 1), (1, 0)])
+
+    def exchange(value, axis):
+        return lax.all_to_all(value, axis, split_axis=0, concat_axis=0, tiled=True)
+
+    def in_order(kept, got):
+        return jnp.concatenate(
+            [jnp.where(first_core, kept, got), jnp.where(first_core, got, kept)], axis=0
+        )
+
+    def own_subs(value):
+        return jnp.stack(
+            [
+                lax.dynamic_slice_in_dim(value, 2 * q * sub + occ_index * sub, sub, 2)
+                for q in range(quarters)
+            ]
+        )
+
+    singles_all = lax.all_gather(trial_singles, "root", axis=0, tiled=True)
+    other_doubles = swap(trial_doubles)
+    trial_piece = exchange(in_order(own_subs(trial_doubles), own_subs(other_doubles)), "root")
+    trial_piece = trial_piece.reshape(root_count, virt_local, sub)
+    slabs = jnp.stack(jnp.split(trial_doubles, virt_groups, axis=2))
+    slabs = exchange(slabs, "virt")
+
+    singles_cols = lax.dynamic_slice_in_dim(singles_all, own_start, occ_half, 1)
+    outer_kept, outer_sent = outer_terms(core, singles_cols, w_ovoo)
+    outer_sum = (outer_kept + swap(outer_sent).astype(jnp.float32)).astype(jnp.bfloat16)
+    outer_quarters = exchange(
+        outer_sum.reshape(root_groups, local_roots, virt_local, sub), "root"
+    )
+
+    fock_cols = lax.dynamic_slice_in_dim(occ_fock, own_start, occ_half, 1)
+    occ_sum = occ_terms(
+        trial_doubles.reshape(local_roots * virt_local, pair_local),
+        other_doubles.reshape(local_roots * virt_local, pair_local),
+        lax.dynamic_slice_in_dim(fock_cols, own_start, occ_half, 0),
+        lax.dynamic_slice_in_dim(fock_cols, other_start, occ_half, 0),
+        occ_fock,
+    ).reshape(local_roots, virt_local, pair_local)
+    vv_term = exchange(virt_product(virt_fock, slabs), "virt")
+
+    partial_coupling = coupling_sums(core, trial_piece, swap(trial_piece), w_ooov)
+    coupling_part = lax.dynamic_update_slice(
+        jnp.zeros((root_count, occ_count), jnp.float32), partial_coupling, (jnp.int32(0), own_start)
+    )
+
+    outer_mine = lax.dynamic_slice_in_dim(outer_quarters, quarters * occ_index, quarters)
+    outer_theirs = swap(
+        lax.dynamic_slice_in_dim(outer_quarters, quarters * (1 - occ_index), quarters)
+    )
+    sigma_doubles, sigma_kept, sigma_sent = sigma_terms(
+        core, own_active, vv_term, outer_mine, outer_theirs, occ_sum
+    )
+    sigma_piece = exchange(in_order(sigma_kept, swap(sigma_sent)), "root")
+    doubles_piece = project(trial_piece, sigma_piece.reshape(root_count, virt_local, sub))
+
+    coupling, doubles_part = lax.psum((coupling_part, doubles_piece), ("root", "virt", "occ"))
+    singles_fock = jnp.dot(singles_all, occ_fock, preferred_element_type=jnp.float32)
+    singles_every = active[:, None] * (-singles_fock - 0.5 * coupling)
+    sigma_singles = lax.dynamic_slice_in_dim(singles_every, root_index * local_roots, local_roots)
+    singles_part = jnp.dot(
+        singles_all.astype(jnp.float32), singles_every.T, precision=lax.Precision.HIGHEST
+    )
+    whole_matrix = doubles_part / math.sqrt(
+        occ_count * occ_count * virt_count
+    ) + singles_part / math.sqrt(occ_count)
+    subspace = lax.dynamic_slice_in_dim(whole_matrix, root_index * local_roots, local_roots, 0)
+    return (sigma_doubles, sigma_singles, subspace)
+
+
 def solution(mesh):
     placed = (
         P("root", None),

time: 599 us -> 343 us (0.57)
  local copies, waits for them, and re-layouts: 192 us -> 24.9 us
  waiting for transfers between devices: 264 us -> 111 us
  Pallas kernels: 0 us -> 121 us
  matrix products: 36.1 us -> 0.19 us
  between operations: 14.8 us -> 0.9 us
  starting transfers between devices: 28.3 us -> 20.7 us
    all_to_all x6 -> x5, waiting for transfers between devices: 263 us -> 103 us  [exchange(): return lax.all_to_all(value, axis, split_axis=0, concat_axis=0, tiled=True)]
    pallas_call x0 -> x6, Pallas kernels: none -> 121 us  [the longest x1 71.3 us: occ_terms(): call(body, (count,), [whole, whole, fock_spec, fock_spec, pl.BlockSpec(un...]
    unnamed x23 -> x22, local copies, waits for them, and re-layouts: 74 us -> 6.29 us
    all_to_all x5 -> x0, local copies, waits for them, and re-layouts: 42.2 us -> none  [the longest x1 14.5 us: local(): lax.all_to_all(outer_part, 'root', split_axis=0, concat_axis=2, tiled=True)]
    reshape x6 -> x4, local copies, waits for them, and re-layouts: 45 us -> 2.9 us  [the longest x2 2.5 us: same_row(): table.reshape(left, rows, right, rows) * eye[None, :, None, :]]
    dot_general x6 -> x0, matrix products: 35.9 us -> none  [the longest x2 14.6 us: flat_pairs(): lax.dot_general(left.reshape(left.shape[0], -1), right.reshape(right.shap...]
    all_gather x1 -> x0, local copies, waits for them, and re-layouts: 12.7 us -> none  [local(): gathered = lax.all_gather(trial_doubles, 'occ', axis=2, tiled=True)]
    convert_element_type x2 -> x0, local copies, waits for them, and re-layouts: 12 us -> none  [the longest x1 8.92 us: local(): vv_value = vv_term.astype(jnp.float32)]
  transfers between devices with their start and end apart: 8 -> 10, of which waited for: 4 -> 6; matrix products, arithmetic and copies ran while one was open for 37% -> 9% of each run, Pallas kernels for 0% -> 29%
where the time goes in v1:
time: 343 us; the launch traced here: 341 us
  Pallas kernels  121 us (35%)
  waiting for transfers between devices  111 us (32%)
  blocking collectives  49.7 us (14%)
  local copies, waits for them, and re-layouts  24.9 us (7%)
  starting transfers between devices  20.7 us (6%)
  other arithmetic  13.5 us (4%)
    all_to_all x5, waiting for transfers between devices, exchange(): return lax.all_to_all(value, axis, split_axis=0, concat_axis=0, tiled=True)  103 us
    pallas_call x1, Pallas kernels, occ_terms(): call(body, (count,), [whole, whole, fock_spec, fock_spec, pl.BlockSpec(un...  71.3 us
    psum x1, blocking collectives, local(): lax.psum((coupling_part, doubles_piece), ('root', 'virt', 'occ'))  36.9 us
    all_to_all x5, starting transfers between devices, exchange(): return lax.all_to_all(value, axis, split_axis=0, concat_axis=0, tiled=True)  20.6 us
    pallas_call x1, Pallas kernels, outer_terms(): call(outer_body, (virt_local // ROWS,), [SCALAR, pl.BlockSpec(mix.shape,...  18.5 us
    pallas_call x1, Pallas kernels, coupling_sums(): call(coupling_body, (virt_local // ROWS,), [SCALAR, piece, piece, pl.Bloc...  18 us
    all_gather x1, blocking collectives, local(): singles_all = lax.all_gather(trial_singles, 'root', axis=0, tiled=True)  12.8 us
    ppermute x5, waiting for transfers between devices, swap(): return lax.ppermute(value, 'occ', [(0, 1), (1, 0)])  7.05 us
  transfers between devices with their start and end apart: 10, of which 6 were waited for; matrix products, arithmetic and copies ran while one was open for 9% of the time, Pallas kernels for 29%

profile of v1, /device:TPU:0, one launch (start us, length us, event | category | flops | bytes accessed | tf_op | source)
XLA Modules:
  0.0 341.2 jit_solution(6855647780041188679)
XLA Ops:
  0.7 12.8 %all-gather = bf16[4,2,96]{2,1,0:T(2,128)(2,1)S(1)} all-gather(bf16[1,2,96]{2,1,0:T(2,128)(2,1)} %bitcast.48), channel_id=1, replica_groups=mesh['root'=4,'virt'=4,'occ'=2] {'root'}, dimensions={0}, use_global_device_ids=true | all-gather | bytes 1920 | tf_op jit(solution)/shard_map/all_gather | solution.py:410
  14.5 18.5 %shard_map.95 = (f32[8,120,1152]{2,1,0:T(8,128)}, bf16[8,120,1152]{2,1,0:T(8,128)(2,1)}) custom-call(s32[1]{0:T(128)} %bitcast.core, bf16[64,384]{1,0:T(8,128)(2,1)S(1)} %mul.92.mix, bf16[48,120,2304]{2,1,0:T(8,128)(2,1)} %weights.2), custom_call_target="tpu_custom_call" | custom-call | flops 1698693120 | bytes 26542080 | tf_op jit(solution)/shard_map/pallas_call | solution.py:131
  34.2 1.7 pad_maximum_fusion
  35.9 3.7 %all-to-all-start = ((bf16[4,2,120,1152]{3,2,1,0:T(8,128)(2,1)}), bf16[4,2,120,1152]{3,2,1,0:T(8,128)(2,1)S(1)}, u32[]{:S(2)}, u32[]{:S(2)}) async-start(bf16[4,2,120,1152]{3,2,1,0:T(8,128)(2,1)} %pad_maximum_fusion), calls=%async_computation | async-start | bytes 4423680 | tf_op jit(solution)/shard_map/all_to_all | solution.py:395
  39.6 4.8 %add_convert_fusion = bf16[8,120,1152]{2,1,0:T(8,128)(2,1)} fusion(f32[8,120,1152]{2,1,0:T(8,128)} %get-tuple-element.8, bf16[8,120,1152]{2,1,0:T(8,128)(2,1)} %collective-permute-done), kind=kLoop, calls=%fused_computation | loop fusion | flops 3317760 | bytes 8847360 | tf_op jit(solution)/shard_map/convert_element_type | solution.py:419
  44.4 22.1 %all-to-all-done.amps = bf16[4,2,120,1152]{3,2,1,0:T(8,128)(2,1)S(1)} async-done(((bf16[4,2,120,1152]{3,2,1,0:T(8,128)(2,1)}), bf16[4,2,120,1152]{3,2,1,0:T(8,128)(2,1)S(1)}, u32[]{:S(2)}, u32[]{:S(2)}) %all-to-all-start) | async-done | bytes 2211872 | tf_op jit(solution)/shard_map/all_to_all | solution.py:395
  66.6 4.6 %all-to-all-start.2 = ((bf16[4,2,120,1152]{3,2,1,0:T(8,128)(2,1)}), bf16[4,2,120,1152]{3,2,1,0:T(8,128)(2,1)}, u32[]{:S(2)}, u32[]{:S(2)}) async-start(bf16[4,2,120,1152]{3,2,1,0:T(8,128)(2,1)} %bitcast.43), calls=%async_computation.2 | async-start | bytes 4423680 | tf_op jit(solution)/shard_map/all_to_all | solution.py:395
  72.7 3.9 %shard_map.94 = bf16[4,2,120,1152]{3,2,1,0:T(8,128)(2,1)} custom-call(bf16[4,4,120,120]{3,2,1,0:T(8,128)(2,1)S(1)} %bitcast.42, bf16[4,2,120,1152]{3,2,1,0:T(8,128)(2,1)S(1)} %all-to-all-done.amps), custom_call_target="tpu_custom_call" | custom-call | flops 1061683200 | bytes 4423680 | tf_op jit(solution)/shard_map/pallas_call | solution.py:301
  76.7 45.2 %all-to-all-done.2 = bf16[4,2,120,1152]{3,2,1,0:T(8,128)(2,1)} async-done(((bf16[4,2,120,1152]{3,2,1,0:T(8,128)(2,1)}), bf16[4,2,120,1152]{3,2,1,0:T(8,128)(2,1)}, u32[]{:S(2)}, u32[]{:S(2)}) %all-to-all-start.2) | async-done | bytes 2211872 | tf_op jit(solution)/shard_map/all_to_all | solution.py:395
  121.9 3.6 %all-to-all-start.1 = ((bf16[4,2,120,1152]{3,2,1,0:T(8,128)(2,1)}), bf16[4,2,120,1152]{3,2,1,0:T(8,128)(2,1)S(1)}, u32[]{:S(2)}, u32[]{:S(2)}) async-start(bf16[4,2,120,1152]{3,2,1,0:T(8,128)(2,1)} %shard_map.94), calls=%async_computation.1 | async-start | bytes 4423680 | tf_op jit(solution)/shard_map/all_to_all | solution.py:395
  126.0 1.8 reshape_reshape.6.refs_2_
  128.1 1.8 reshape_reshape.7.refs_3_
  129.9 2.1 mul.99.refs_5_
  133.9 1.3 dynamic-slice_bitcast_fusion.1
  135.6 1.6 pad_maximum_fusion.1
  137.2 2.7 constant_dynamic-slice_fusion.2
  140.0 11.2 %all-to-all-done.1.vv = bf16[4,2,120,1152]{3,2,1,0:T(8,128)(2,1)S(1)} async-done(((bf16[4,2,120,1152]{3,2,1,0:T(8,128)(2,1)}), bf16[4,2,120,1152]{3,2,1,0:T(8,128)(2,1)S(1)}, u32[]{:S(2)}, u32[]{:S(2)}) %all-to-all-start.1) | async-done | bytes 2211872 | tf_op jit(solution)/shard_map/all_to_all | solution.py:395
  151.1 1.4 copy-done.5
  152.5 3.6 %all-to-all-start.3 = ((bf16[4,2,120,1152]{3,2,1,0:T(8,128)(2,1)}), bf16[4,2,120,1152]{3,2,1,0:T(8,128)(2,1)S(1)}, u32[]{:S(2)}, u32[]{:S(2)}) async-start(bf16[4,2,120,1152]{3,2,1,0:T(8,128)(2,1)} %pad_maximum_fusion.1), calls=%async_computation.3 | async-start | bytes 4423680 | tf_op jit(solution)/shard_map/all_to_all | solution.py:395
  156.1 1.6 copy-done.1
  161.1 71.3 %shard_map.96 = f32[240,4608]{1,0:T(8,128)} custom-call(bf16[240,4608]{1,0:T(8,128)(2,1)S(1)} %bitcast.41, bf16[240,4608]{1,0:T(8,128)(2,1)} %bitcast.10.refs_1_, f32[12,4,4608]{2,1,0:T(4,128)S(1)} %copy-done.2, f32[12,4,4608]{2,1,0:T(4,128)S(1)} %copy-done.3, f32[96,384]{1,0:T(8,128)S(1)} %tile.10.refs_4_, bf16[384,384]{1,0:T(8,128)(2,1)S(1)} %copy-done.4), custom_call_target="tpu_custom_call" | custom-call | flops 20384317440 | bytes 8847360 | tf_op jit(solution)/shard_map/pallas_call | solution.py:270
  232.3 5.5 %shard_map.97 = (bf16[2,120,4608]{2,1,0:T(8,128)(2,1)}, bf16[2,2,120,1152]{3,2,1,0:T(8,128)(2,1)S(1)}, bf16[2,2,120,1152]{3,2,1,0:T(8,128)(2,1)S(1)}) custom-call(s32[1]{0:T(128)} %bitcast.core, f32[2]{0:T(128)S(1)} %dynamic_slice.37.active, bf16[4,2,120,1152]{3,2,1,0:T(8,128)(2,1)} %copy-done.5, bf16[2,2,120,1152]{3,2,1,0:T(8,128)(2,1)S(1)} %get-tuple-element.28.mine, ...), custom_call_target="tpu_custom_call" | custom-call | flops 8847360 | bytes 15482880 | tf_op jit(solution)/shard_map/pallas_call | solution.py:332
  237.8 2.7 collective-permute-done.4
  240.8 1.6 pad_maximum_fusion.2
  242.4 5.1 %all-to-all-start.4 = ((bf16[4,2,120,1152]{3,2,1,0:T(8,128)(2,1)}), bf16[4,2,120,1152]{3,2,1,0:T(8,128)(2,1)}, u32[]{:S(2)}, u32[]{:S(2)}) async-start(bf16[4,2,120,1152]{3,2,1,0:T(8,128)(2,1)} %pad_maximum_fusion.2), calls=%async_computation.4 | async-start | bytes 4423680 | tf_op jit(solution)/shard_map/all_to_all | solution.py:395
  247.5 4.3 %collective-permute-done.3.other = bf16[8,120,1152]{2,1,0:T(8,128)(2,1)S(1)} collective-permute-done((bf16[8,120,1152]{2,1,0:T(8,128)(2,1)S(1)}, bf16[8,120,1152]{2,1,0:T(8,128)(2,1)S(1)}, u32[]{:S(2)}, u32[]{:S(2)}) %collective-permute-start.3) | collective-permute-done | bytes 2211872 | tf_op jit(solution)/shard_map/ppermute | solution.py:392
  251.8 18.0 %shard_map.98 = f32[64,384]{1,0:T(8,128)S(1)} custom-call(s32[1]{0:T(128)} %bitcast.core, bf16[8,120,1152]{2,1,0:T(8,128)(2,1)S(1)} %bitcast.39, bf16[8,120,1152]{2,1,0:T(8,128)(2,1)S(1)} %collective-permute-done.3.other, bf16[48,120,2304]{2,1,0:T(8,128)(2,1)} %weights.3), custom_call_target="tpu_custom_call" | custom-call | flops 1698693120 | bytes 26542080 | tf_op jit(solution)/shard_map/pallas_call | solution.py:182
  269.8 2.0 reshape.95
  271.8 1.6 multiply_reduce_fusion
  273.7 24.9 %all-to-all-done.4 = bf16[4,2,120,1152]{3,2,1,0:T(8,128)(2,1)} async-done(((bf16[4,2,120,1152]{3,2,1,0:T(8,128)(2,1)}), bf16[4,2,120,1152]{3,2,1,0:T(8,128)(2,1)}, u32[]{:S(2)}, u32[]{:S(2)}) %all-to-all-start.4) | async-done | bytes 2211872 | tf_op jit(solution)/shard_map/all_to_all | solution.py:395
  298.6 3.6 %shard_map.99 = f32[320,320]{1,0:T(8,128)S(1)} custom-call(bf16[8,120,1152]{2,1,0:T(8,128)(2,1)S(1)} %bitcast.40, bf16[8,120,1152]{2,1,0:T(8,128)(2,1)} %bitcast.17.right), custom_call_target="tpu_custom_call" | custom-call | flops 707788800 | bytes 4423680 | tf_op jit(solution)/shard_map/pallas_call | solution.py:215
  302.9 36.9 %all-reduce = (f32[8,96]{1,0:T(8,128)S(1)}, f32[8,8]{1,0:T(8,128)S(1)}) all-reduce(f32[8,96]{1,0:T(8,128)S(1)} %dynamic_update_slice.3, f32[8,8]{1,0:T(8,128)S(1)} %multiply_reduce_fusion.1), channel_id=1, replica_groups=mesh['root'=4,'virt'=4,'occ'=2] {'root','virt','occ'}, use_global_device_ids=true, to_apply=%region_1.2 | all-reduce | flops 832 | bytes 6656 | tf_op jit(solution)/shard_map/psum | solution.py:449
  (58 shorter events, 12.6 us)
Async XLA Ops:
  14.4 18.5 %copy-start = (bf16[2,120,4608]{2,1,0:T(8,128)(2,1)S(1)}, bf16[2,120,4608]{2,1,0:T(8,128)(2,1)}, u32[]{:S(2)}) copy-start(bf16[2,120,4608]{2,1,0:T(8,128)(2,1)} %param.8) | copy-start | bytes 6635524
  32.9 6.7 %collective-permute-start = (bf16[8,120,1152]{2,1,0:T(8,128)(2,1)}, bf16[8,120,1152]{2,1,0:T(8,128)(2,1)}, u32[]{:S(2)}, u32[]{:S(2)}) collective-permute-start(bf16[8,120,1152]{2,1,0:T(8,128)(2,1)} %get-tuple-element.9), channel_id=1, source_target_pairs={{0,1},{1,0},{2,3},{3,2},{4,5},{5,4},{6,7},{7,6},{8,9},{9,8},{10,11... | collective-permute-start | bytes 6635528 | tf_op jit(solution)/shard_map/ppermute | solution.py:392
  35.9 30.7 %all-to-all-start = ((bf16[4,2,120,1152]{3,2,1,0:T(8,128)(2,1)}), bf16[4,2,120,1152]{3,2,1,0:T(8,128)(2,1)S(1)}, u32[]{:S(2)}, u32[]{:S(2)}) async-start(bf16[4,2,120,1152]{3,2,1,0:T(8,128)(2,1)} %pad_maximum_fusion), calls=%async_computation | async-start | bytes 4423680 | tf_op jit(solution)/shard_map/all_to_all | solution.py:395
  66.6 4.7 %copy-start.8 = (bf16[480,480]{1,0:T(8,128)(2,1)S(1)}, bf16[480,480]{1,0:T(8,128)(2,1)}, u32[]{:S(2)}) copy-start(bf16[480,480]{1,0:T(8,128)(2,1)} %param.10) | copy-start | bytes 1382404
  66.6 5.2 %copy-start.9 = (bf16[96,96]{1,0:T(8,128)(2,1)S(1)}, bf16[96,96]{1,0:T(8,128)(2,1)}, u32[]{:S(2)}) copy-start(bf16[96,96]{1,0:T(8,128)(2,1)} %param.9) | copy-start | bytes 55300
  66.6 55.3 %all-to-all-start.2 = ((bf16[4,2,120,1152]{3,2,1,0:T(8,128)(2,1)}), bf16[4,2,120,1152]{3,2,1,0:T(8,128)(2,1)}, u32[]{:S(2)}, u32[]{:S(2)}) async-start(bf16[4,2,120,1152]{3,2,1,0:T(8,128)(2,1)} %bitcast.43), calls=%async_computation.2 | async-start | bytes 4423680 | tf_op jit(solution)/shard_map/all_to_all | solution.py:395
  71.2 62.7 %collective-permute-start.2 = (bf16[2,120,4608]{2,1,0:T(8,128)(2,1)}, bf16[2,120,4608]{2,1,0:T(8,128)(2,1)}, u32[]{:S(2)}, u32[]{:S(2)}) collective-permute-start(bf16[2,120,4608]{2,1,0:T(8,128)(2,1)} %param.8), channel_id=1, source_target_pairs={{0,1},{1,0},{2,3},{3,2},{4,5},{5,4},{6,7},{7,6},{8,9},{9,8},{10,11... | collective-permute-start | bytes 6635528 | tf_op jit(solution)/shard_map/ppermute | solution.py:392
  121.9 29.2 %all-to-all-start.1 = ((bf16[4,2,120,1152]{3,2,1,0:T(8,128)(2,1)}), bf16[4,2,120,1152]{3,2,1,0:T(8,128)(2,1)S(1)}, u32[]{:S(2)}, u32[]{:S(2)}) async-start(bf16[4,2,120,1152]{3,2,1,0:T(8,128)(2,1)} %shard_map.94), calls=%async_computation.1 | async-start | bytes 4423680 | tf_op jit(solution)/shard_map/all_to_all | solution.py:395
  127.8 6.0 %copy-start.10 = (s32[8]{0:T(128)S(1)}, s32[8]{0:T(128)}, u32[]{:S(2)}) copy-start(s32[8]{0:T(128)} %param.13) | copy-start | bytes 100
  129.9 5.3 %copy-start.6 = (bf16[1,2,120,1152]{3,2,1,0:T(8,128)(2,1)S(1)}, bf16[1,2,120,1152]{3,2,1,0:T(8,128)(2,1)}, u32[]{:S(2)}) copy-start(bf16[1,2,120,1152]{3,2,1,0:T(8,128)(2,1)} %get-tuple-element.19) | copy-start | bytes 1658884
  129.9 5.3 %copy-start.7 = (bf16[1,2,120,1152]{3,2,1,0:T(8,128)(2,1)S(1)}, bf16[1,2,120,1152]{3,2,1,0:T(8,128)(2,1)}, u32[]{:S(2)}) copy-start(bf16[1,2,120,1152]{3,2,1,0:T(8,128)(2,1)} %get-tuple-element.24) | copy-start | bytes 1658884
  139.9 92.4 %collective-permute-start.1 = (bf16[2,2,120,1152]{3,2,1,0:T(8,128)(2,1)}, bf16[2,2,120,1152]{3,2,1,0:T(8,128)(2,1)}, u32[]{:S(2)}, u32[]{:S(2)}) collective-permute-start(bf16[2,2,120,1152]{3,2,1,0:T(8,128)(2,1)} %get-tuple-element.27), channel_id=1, source_target_pairs={{0,1},{1,0},{2,3},{3,2},{4,5},{5,4},{6,7},{7,6},{8,9},{9,8},{10,11... | collective-permute-start | bytes 3317768 | tf_op jit(solution)/shard_map/ppermute | solution.py:392
  151.1 1.4 copy-start.5
  152.5 89.9 %all-to-all-start.3 = ((bf16[4,2,120,1152]{3,2,1,0:T(8,128)(2,1)}), bf16[4,2,120,1152]{3,2,1,0:T(8,128)(2,1)S(1)}, u32[]{:S(2)}, u32[]{:S(2)}) async-start(bf16[4,2,120,1152]{3,2,1,0:T(8,128)(2,1)} %pad_maximum_fusion.1), calls=%async_computation.3 | async-start | bytes 4423680 | tf_op jit(solution)/shard_map/all_to_all | solution.py:395
  156.1 1.6 copy-start.1
  157.8 1.2 copy-start.2
  158.9 1.2 copy-start.3
  160.1 1.0 copy-start.4
  237.8 2.7 collective-permute-start.4
  242.4 56.2 %all-to-all-start.4 = ((bf16[4,2,120,1152]{3,2,1,0:T(8,128)(2,1)}), bf16[4,2,120,1152]{3,2,1,0:T(8,128)(2,1)}, u32[]{:S(2)}, u32[]{:S(2)}) async-start(bf16[4,2,120,1152]{3,2,1,0:T(8,128)(2,1)} %pad_maximum_fusion.2), calls=%async_computation.4 | async-start | bytes 4423680 | tf_op jit(solution)/shard_map/all_to_all | solution.py:395
  247.4 4.3 %collective-permute-start.3 = (bf16[8,120,1152]{2,1,0:T(8,128)(2,1)S(1)}, bf16[8,120,1152]{2,1,0:T(8,128)(2,1)S(1)}, u32[]{:S(2)}, u32[]{:S(2)}) collective-permute-start(bf16[8,120,1152]{2,1,0:T(8,128)(2,1)S(1)} %bitcast.38), channel_id=1, source_target_pairs={{0,1},{1,0},{2,3},{3,2},{4,5},{5,4},{6,7},{7,6},{8,9},{9,8},{10,11... | collective-permute-start | bytes 6635528 | tf_op jit(solution)/shard_map/ppermute | solution.py:392

commit v2 on v1

--- a/solution.py
+++ b/solution.py
@@ -225,8 +225,8 @@
     return same_row(table, roots, rows, roots)
 
 
-def occ_body(tile, count, own, other, own_fock, other_fock, unit, second, out):
-    column = pl.program_id(0)
+def occ_body(tile, count, first, own, other, own_fock, other_fock, unit, second, out):
+    column = pl.program_id(0) + first
 
     def spread(rows):
         parts = [unit[...] * rows[k : k + 1, :] for k in range(rows.shape[0])]
@@ -246,12 +246,14 @@
     out[...] = lax.fori_loop(0, count, step, begin)
 
 
-def occ_terms(own, other, fock_own, fock_other, occ_fock):
+def occ_terms(own, other, fock_own, fock_other, occ_fock, part, parts):
     rows, pairs = own.shape
     occ_count = occ_fock.shape[0]
     group = 128 // math.gcd(occ_count, 128)
     tile = group * occ_count
     count = pairs // tile
+    steps = count // parts
+    first = part * steps
     eye = jnp.eye(occ_count, dtype=jnp.float32)
     unit = jnp.tile(eye, (1, group))
     second = (
@@ -262,14 +264,14 @@
         return jnp.repeat(block.astype(jnp.float32), occ_count, axis=1).reshape(count, group, pairs)
 
     whole = pl.BlockSpec((rows, pairs), lambda c: (0, 0))
-    fock_spec = pl.BlockSpec((count, group, tile), lambda c: (0, 0, c))
+    fock_spec = pl.BlockSpec((count, group, tile), lambda c: (0, 0, c + first))
 
     def body(*refs):
-        occ_body(tile, count, *refs)
+        occ_body(tile, count, first, *refs)
 
     return call(
         body,
-        (count,),
+        (steps,),
         [
             whole,
             whole,
@@ -279,8 +281,8 @@
             pl.BlockSpec(second.shape, lambda c: (0, 0)),
         ],
         pl.BlockSpec((rows, tile), lambda c: (0, c)),
-        jax.ShapeDtypeStruct((rows, pairs), jnp.float32),
-        flops=4 * rows * pairs * pairs,
+        jax.ShapeDtypeStruct((rows, steps * tile), jnp.float32),
+        flops=8 * rows * pairs * pairs // parts,
         moved=8 * rows * pairs,
     )(own, other, wide(fock_own), wide(fock_other), unit, second)
 
@@ -363,7 +365,7 @@
         and virt_local % ROWS == 0
         and sub % 128 == 0
         and sub * lax.axis_size("virt") == pair_local
-        and pair_local % tile == 0
+        and pair_local % (2 * tile) == 0
     )
 
 
@@ -416,20 +418,35 @@
 
     singles_cols = lax.dynamic_slice_in_dim(singles_all, own_start, occ_half, 1)
     outer_kept, outer_sent = outer_terms(core, singles_cols, w_ovoo)
+    outer_kept, outer_sent, slabs = lax.optimization_barrier((outer_kept, outer_sent, slabs))
     outer_sum = (outer_kept + swap(outer_sent).astype(jnp.float32)).astype(jnp.bfloat16)
+    fock_cols = lax.dynamic_slice_in_dim(occ_fock, own_start, occ_half, 1)
     outer_quarters = exchange(
         outer_sum.reshape(root_groups, local_roots, virt_local, sub), "root"
     )
 
-    fock_cols = lax.dynamic_slice_in_dim(occ_fock, own_start, occ_half, 1)
-    occ_sum = occ_terms(
-        trial_doubles.reshape(local_roots * virt_local, pair_local),
-        other_doubles.reshape(local_roots * virt_local, pair_local),
-        lax.dynamic_slice_in_dim(fock_cols, own_start, occ_half, 0),
-        lax.dynamic_slice_in_dim(fock_cols, other_start, occ_half, 0),
-        occ_fock,
-    ).reshape(local_roots, virt_local, pair_local)
-    vv_term = exchange(virt_product(virt_fock, slabs), "virt")
+    own_flat = trial_doubles.reshape(local_roots * virt_local, pair_local)
+    other_flat = other_doubles.reshape(local_roots * virt_local, pair_local)
+
+    def occ_part(cols, part):
+        return occ_terms(
+            own_flat,
+            other_flat,
+            lax.dynamic_slice_in_dim(cols, own_start, occ_half, 0),
+            lax.dynamic_slice_in_dim(cols, other_start, occ_half, 0),
+            occ_fock,
+            part,
+            2,
+        )
+
+    occ_low = occ_part(fock_cols, 0)
+    product = virt_product(virt_fock, slabs)
+    product, occ_low, outer_quarters = lax.optimization_barrier((product, occ_low, outer_quarters))
+    vv_term = exchange(product, "virt")
+    vv_term, fock_cols = lax.optimization_barrier((vv_term, fock_cols))
+    occ_high = occ_part(fock_cols, 1)
+    occ_sum = jnp.concatenate([occ_low, occ_high], axis=1)
+    occ_sum = occ_sum.reshape(local_roots, virt_local, pair_local)
 
     partial_coupling = coupling_sums(core, trial_piece, swap(trial_piece), w_ooov)
     coupling_part = lax.dynamic_update_slice(
@@ -446,7 +463,9 @@
     sigma_piece = exchange(in_order(sigma_kept, swap(sigma_sent)), "root")
     doubles_piece = project(trial_piece, sigma_piece.reshape(root_count, virt_local, sub))
 
-    coupling, doubles_part = lax.psum((coupling_part, doubles_piece), ("root", "virt", "occ"))
+    partial = jnp.concatenate([coupling_part, doubles_piece], axis=1)
+    partial = jnp.sum(lax.all_gather(partial, ("root", "virt", "occ")), axis=0)
+    coupling, doubles_part = partial[:, :occ_count], partial[:, occ_count:]
     singles_fock = jnp.dot(singles_all, occ_fock, preferred_element_type=jnp.float32)
     singles_every = active[:, None] * (-singles_fock - 0.5 * coupling)
     sigma_singles = lax.dynamic_slice_in_dim(singles_every, root_index * local_roots, local_roots)

time: 343 us -> 308 us (0.90)
  waiting for transfers between devices: 111 us -> 56 us
  local copies, waits for them, and re-layouts: 24.9 us -> 37.9 us
  starting transfers between devices: 20.7 us -> 24.6 us
    all_to_all x5, waiting for transfers between devices: 103 us -> 44.9 us  [exchange(): return lax.all_to_all(value, axis, split_axis=0, concat_axis=0, tiled=True)]
    all_gather x0 -> x1, blocking collectives: none -> 39 us  [local(): partial = jnp.sum(lax.all_gather(partial, ('root', 'virt', 'occ')), axis=0)]
    psum x1 -> x0, blocking collectives: 36.9 us -> none  [local(): lax.psum((coupling_part, doubles_piece), ('root', 'virt', 'occ'))]
    another operation x2 -> x4, local copies, waits for them, and re-layouts: 3.53 us -> 11.9 us  [wide(): jnp.repeat(block.astype(jnp.float32), occ_count, axis=1)]
    broadcast_in_dim x2 -> x4, local copies, waits for them, and re-layouts: 0.72 us -> 5.53 us  [wide(): jnp.repeat(block.astype(jnp.float32), occ_count, axis=1)]
    ppermute x5, waiting for transfers between devices: 7.05 us -> 11.1 us  [swap(): return lax.ppermute(value, 'occ', [(0, 1), (1, 0)])]
    all_to_all x5, starting transfers between devices: 20.6 us -> 24.1 us  [exchange(): return lax.all_to_all(value, axis, split_axis=0, concat_axis=0, tiled=True)]
    pallas_call x1 -> x2, Pallas kernels: 71.3 us -> 73.9 us  [occ_terms(): call(body, (steps,), [whole, whole, fock_spec, fock_spec, pl.BlockSpec(un...]
  transfers between devices with their start and end apart: 10 -> 10, of which waited for: 6 -> 5; matrix products, arithmetic and copies ran while one was open for 9% -> 13% of each run, Pallas kernels for 29% -> 39%
where the time goes in v2:
time: 308 us; the launch traced here: 307 us
  Pallas kernels  122 us (40%)
  waiting for transfers between devices  56 us (18%)
  blocking collectives  50.1 us (16%)
  local copies, waits for them, and re-layouts  37.9 us (12%)
  starting transfers between devices  24.6 us (8%)
  other arithmetic  14.8 us (5%)
    pallas_call x2, Pallas kernels, occ_terms(): call(body, (steps,), [whole, whole, fock_spec, fock_spec, pl.BlockSpec(un...  73.9 us
    all_to_all x5, waiting for transfers between devices, exchange(): return lax.all_to_all(value, axis, split_axis=0, concat_axis=0, tiled=True)  44.9 us
    all_gather x1, blocking collectives, local(): partial = jnp.sum(lax.all_gather(partial, ('root', 'virt', 'occ')), axis=0)  39 us
    all_to_all x5, starting transfers between devices, exchange(): return lax.all_to_all(value, axis, split_axis=0, concat_axis=0, tiled=True)  24.1 us
    pallas_call x1, Pallas kernels, coupling_sums(): call(coupling_body, (virt_local // ROWS,), [SCALAR, piece, piece, pl.Bloc...  18 us
    pallas_call x1, Pallas kernels, outer_terms(): call(outer_body, (virt_local // ROWS,), [SCALAR, pl.BlockSpec(mix.shape,...  17.2 us
    another operation x4, local copies, waits for them, and re-layouts, wide(): jnp.repeat(block.astype(jnp.float32), occ_count, axis=1)  11.9 us
    all_gather x1, blocking collectives, local(): singles_all = lax.all_gather(trial_singles, 'root', axis=0, tiled=True)  11.1 us
  transfers between devices with their start and end apart: 10, of which 5 were waited for; matrix products, arithmetic and copies ran while one was open for 13% of the time, Pallas kernels for 39%

profile of v2, /device:TPU:0, one launch (start us, length us, event | category | flops | bytes accessed | tf_op | source)
XLA Modules:
  0.0 306.6 jit_solution(1009720144404474384)
XLA Ops:
  0.6 3.1 %dynamic-slice_bitcast_fusion.3 = (bf16[1,2,120,1152]{3,2,1,0:T(8,128)(2,1)}, bf16[1,2,120,1152]{3,2,1,0:T(8,128)(2,1)S(1)}, bf16[1,2,120,1152]{3,2,1,0:T(8,128)...) fusion(bf16[2,120,4608]{2,1,0:T(8,128)(2,1)} %param.8, ...), kind=kLoop, calls=%fused_computation.22 | loop fusion | bytes 6635528 | tf_op jit(solution)/shard_map/stack | solution.py:405
  3.8 1.7 pad_maximum_fusion.1
  5.5 5.3 %all-to-all-start = ((bf16[4,2,120,1152]{3,2,1,0:T(8,128)(2,1)}), bf16[4,2,120,1152]{3,2,1,0:T(8,128)(2,1)S(1)}, u32[]{:S(2)}, u32[]{:S(2)}) async-start(bf16[4,2,120,1152]{3,2,1,0:T(8,128)(2,1)} %pad_maximum_fusion.1), calls=%async_computation | async-start | bytes 4423680 | tf_op jit(solution)/shard_map/all_to_all | solution.py:397
  10.8 11.1 %all-gather.1 = bf16[4,2,96]{2,1,0:T(2,128)(2,1)S(1)} all-gather(bf16[1,2,96]{2,1,0:T(2,128)(2,1)S(1)} %bitcast.51), channel_id=1, replica_groups=mesh['root'=4,'virt'=4,'occ'=2] {'root'}, dimensions={0}, use_global_device_ids=true | all-gather | bytes 1920 | tf_op jit(solution)/shard_map/all_gather | solution.py:412
  22.9 17.2 %shard_map.94 = (f32[8,120,1152]{2,1,0:T(8,128)}, bf16[8,120,1152]{2,1,0:T(8,128)(2,1)S(1)}) custom-call(s32[1]{0:T(128)} %bitcast.core, bf16[64,384]{1,0:T(8,128)(2,1)S(1)} %mul.99.mix, bf16[48,120,2304]{2,1,0:T(8,128)(2,1)} %weights.2), custom_call_target="tpu_custom_call" | custom-call | flops 1698693120 | bytes 26542080 | tf_op jit(solution)/shard_map/pallas_call | solution.py:131
  42.1 4.0 %collective-permute-done.1 = bf16[8,120,1152]{2,1,0:T(8,128)(2,1)S(1)} collective-permute-done((bf16[8,120,1152]{2,1,0:T(8,128)(2,1)}, bf16[8,120,1152]{2,1,0:T(8,128)(2,1)S(1)}, u32[]{:S(2)}, u32[]{:S(2)}) %collective-permute-start.1) | collective-permute-done | bytes 2211872 | tf_op jit(solution)/shard_map/ppermute | solution.py:394
  46.1 4.2 %add_convert_fusion = bf16[8,120,1152]{2,1,0:T(8,128)(2,1)} fusion(f32[8,120,1152]{2,1,0:T(8,128)} %get-tuple-element.19, bf16[8,120,1152]{2,1,0:T(8,128)(2,1)S(1)} %collective-permute-done.1), kind=kLoop, calls=%fused_computation.1 | loop fusion | flops 3317760 | bytes 8847360 | tf_op jit(solution)/shard_map/convert_element_type | solution.py:422
  50.3 4.6 %all-to-all-start.1 = ((bf16[4,2,120,1152]{3,2,1,0:T(8,128)(2,1)}), bf16[4,2,120,1152]{3,2,1,0:T(8,128)(2,1)}, u32[]{:S(2)}, u32[]{:S(2)}) async-start(bf16[4,2,120,1152]{3,2,1,0:T(8,128)(2,1)} %bitcast.45), calls=%async_computation.1 | async-start | bytes 4423680 | tf_op jit(solution)/shard_map/all_to_all | solution.py:397
  56.8 3.0 reshape_reshape.12.refs_2_
  61.2 3.0 reshape_reshape.13.refs_3_
  64.9 4.0 %shard_map.95 = bf16[4,2,120,1152]{3,2,1,0:T(8,128)(2,1)} custom-call(bf16[4,4,120,120]{3,2,1,0:T(8,128)(2,1)S(1)} %bitcast.43, bf16[4,2,120,1152]{3,2,1,0:T(8,128)(2,1)S(1)} %all-to-all-done.amps), custom_call_target="tpu_custom_call" | custom-call | flops 1061683200 | bytes 4423680 | tf_op jit(solution)/shard_map/pallas_call | solution.py:303
  68.9 36.9 %shard_map.96 = f32[240,2304]{1,0:T(8,128)S(1)} custom-call(bf16[240,4608]{1,0:T(8,128)(2,1)} %bitcast.46, bf16[240,4608]{1,0:T(8,128)(2,1)} %bitcast.9.refs_1_, f32[12,4,4608]{2,1,0:T(4,128)S(1)} %copy-done.2, f32[12,4,4608]{2,1,0:T(4,128)S(1)} %copy-done.3, f32[96,384]{1,0:T(8,128)S(1)} %tile.9.refs_4_, bf16[384,384]{1,0:T(8,128)(2,1)S(1)} %mul.104.refs_5_), custom_call_target="tpu_custom_call" | custom-call | flops 20384317440 | bytes 8847360 | tf_op jit(solution)/shard_map/pallas_call | solution.py:272
  107.1 4.3 %all-to-all-start.2 = ((bf16[4,2,120,1152]{3,2,1,0:T(8,128)(2,1)}), bf16[4,2,120,1152]{3,2,1,0:T(8,128)(2,1)S(1)}, u32[]{:S(2)}, u32[]{:S(2)}) async-start(bf16[4,2,120,1152]{3,2,1,0:T(8,128)(2,1)} %shard_map.95), calls=%async_computation.2 | async-start | bytes 4423680 | tf_op jit(solution)/shard_map/all_to_all | solution.py:397
  113.4 1.6 pad_maximum_fusion.2
  115.0 2.8 constant_dynamic-slice_fusion.2
  117.8 20.1 %all-to-all-done.2.vv = bf16[4,2,120,1152]{3,2,1,0:T(8,128)(2,1)S(1)} async-done(((bf16[4,2,120,1152]{3,2,1,0:T(8,128)(2,1)}), bf16[4,2,120,1152]{3,2,1,0:T(8,128)(2,1)S(1)}, u32[]{:S(2)}, u32[]{:S(2)}) %all-to-all-start.2) | async-done | bytes 2211872 | tf_op jit(solution)/shard_map/all_to_all | solution.py:397
  139.2 4.7 %all-to-all-start.3 = ((bf16[4,2,120,1152]{3,2,1,0:T(8,128)(2,1)}), bf16[4,2,120,1152]{3,2,1,0:T(8,128)(2,1)S(1)}, u32[]{:S(2)}, u32[]{:S(2)}) async-start(bf16[4,2,120,1152]{3,2,1,0:T(8,128)(2,1)} %pad_maximum_fusion.2), calls=%async_computation.3 | async-start | bytes 4423680 | tf_op jit(solution)/shard_map/all_to_all | solution.py:397
  145.3 3.0 reshape_reshape.14.refs_2_
  149.7 3.0 reshape_reshape.15.refs_3_
  156.0 37.0 %shard_map.97 = f32[240,2304]{1,0:T(8,128)S(1)} custom-call(bf16[240,4608]{1,0:T(8,128)(2,1)} %bitcast.47, bf16[240,4608]{1,0:T(8,128)(2,1)} %bitcast.9.refs_1_, f32[12,4,4608]{2,1,0:T(4,128)S(1)} %copy-done.4, f32[12,4,4608]{2,1,0:T(4,128)S(1)} %copy-done.5, f32[96,384]{1,0:T(8,128)S(1)} %tile.9.refs_4_, bf16[384,384]{1,0:T(8,128)(2,1)S(1)} %copy-done.7), custom_call_target="tpu_custom_call" | custom-call | flops 20384317440 | bytes 8847360 | tf_op jit(solution)/shard_map/pallas_call | solution.py:272
  193.0 2.6 pad_maximum_fusion
  195.6 5.5 %shard_map.98 = (bf16[2,120,4608]{2,1,0:T(8,128)(2,1)}, bf16[2,2,120,1152]{3,2,1,0:T(8,128)(2,1)S(1)}, bf16[2,2,120,1152]{3,2,1,0:T(8,128)(2,1)S(1)}) custom-call(s32[1]{0:T(128)} %bitcast.core, f32[2]{0:T(128)S(1)} %dynamic_slice.45.active, bf16[4,2,120,1152]{3,2,1,0:T(8,128)(2,1)} %copy-done.9, bf16[2,2,120,1152]{3,2,1,0:T(8,128)(2,1)S(1)} %get-tuple-element.42.mine, ...), custom_call_target="tpu_custom_call" | custom-call | flops 8847360 | bytes 15482880 | tf_op jit(solution)/shard_map/pallas_call | solution.py:334
  201.1 2.7 collective-permute-done.4
  204.1 1.6 pad_maximum_fusion.3
  205.7 5.1 %all-to-all-start.4 = ((bf16[4,2,120,1152]{3,2,1,0:T(8,128)(2,1)}), bf16[4,2,120,1152]{3,2,1,0:T(8,128)(2,1)}, u32[]{:S(2)}, u32[]{:S(2)}) async-start(bf16[4,2,120,1152]{3,2,1,0:T(8,128)(2,1)} %pad_maximum_fusion.3), calls=%async_computation.4 | async-start | bytes 4423680 | tf_op jit(solution)/shard_map/all_to_all | solution.py:397
  210.8 4.3 %collective-permute-done.3.other = bf16[8,120,1152]{2,1,0:T(8,128)(2,1)S(1)} collective-permute-done((bf16[8,120,1152]{2,1,0:T(8,128)(2,1)S(1)}, bf16[8,120,1152]{2,1,0:T(8,128)(2,1)S(1)}, u32[]{:S(2)}, u32[]{:S(2)}) %collective-permute-start.3) | collective-permute-done | bytes 2211872 | tf_op jit(solution)/shard_map/ppermute | solution.py:394
  215.1 18.0 %shard_map.99 = f32[64,384]{1,0:T(8,128)S(1)} custom-call(s32[1]{0:T(128)} %bitcast.core, bf16[8,120,1152]{2,1,0:T(8,128)(2,1)S(1)} %bitcast.41, bf16[8,120,1152]{2,1,0:T(8,128)(2,1)S(1)} %collective-permute-done.3.other, bf16[48,120,2304]{2,1,0:T(8,128)(2,1)} %weights.3), custom_call_target="tpu_custom_call" | custom-call | flops 1698693120 | bytes 26542080 | tf_op jit(solution)/shard_map/pallas_call | solution.py:182
  233.1 2.0 reshape.96
  235.1 1.6 multiply_reduce_fusion
  237.0 24.8 %all-to-all-done.4 = bf16[4,2,120,1152]{3,2,1,0:T(8,128)(2,1)} async-done(((bf16[4,2,120,1152]{3,2,1,0:T(8,128)(2,1)}), bf16[4,2,120,1152]{3,2,1,0:T(8,128)(2,1)}, u32[]{:S(2)}, u32[]{:S(2)}) %all-to-all-start.4) | async-done | bytes 2211872 | tf_op jit(solution)/shard_map/all_to_all | solution.py:397
  261.8 3.6 %shard_map.100 = f32[320,320]{1,0:T(8,128)S(1)} custom-call(bf16[8,120,1152]{2,1,0:T(8,128)(2,1)S(1)} %bitcast.42, bf16[8,120,1152]{2,1,0:T(8,128)(2,1)} %bitcast.17.right), custom_call_target="tpu_custom_call" | custom-call | flops 707788800 | bytes 4423680 | tf_op jit(solution)/shard_map/pallas_call | solution.py:215
  266.2 39.0 %all-gather = f32[256,104]{1,0:T(8,128)S(1)} all-gather(f32[8,104]{1,0:T(8,128)S(1)} %pad_maximum_fusion.6), channel_id=2, replica_groups=mesh['root'=4,'virt'=4,'occ'=2] {'root','virt','occ'}, dimensions={0}, use_global_device_ids=true | all-gather | bytes 109824 | tf_op jit(solution)/shard_map/all_gather | solution.py:467
  (80 shorter events, 20.2 us)
Async XLA Ops:
  5.5 5.3 %copy-start.15 = (bf16[2,96]{1,0:T(2,128)(2,1)S(1)}, bf16[2,96]{1,0:T(2,128)(2,1)}, u32[]{:S(2)}) copy-start(bf16[2,96]{1,0:T(2,128)(2,1)} %param.7) | copy-start | bytes 1156
  5.5 36.1 %all-to-all-start = ((bf16[4,2,120,1152]{3,2,1,0:T(8,128)(2,1)}), bf16[4,2,120,1152]{3,2,1,0:T(8,128)(2,1)S(1)}, u32[]{:S(2)}, u32[]{:S(2)}) async-start(bf16[4,2,120,1152]{3,2,1,0:T(8,128)(2,1)} %pad_maximum_fusion.1), calls=%async_computation | async-start | bytes 4423680 | tf_op jit(solution)/shard_map/all_to_all | solution.py:397
  40.1 1.4 copy-start.8
  41.5 4.5 %collective-permute-start.1 = (bf16[8,120,1152]{2,1,0:T(8,128)(2,1)}, bf16[8,120,1152]{2,1,0:T(8,128)(2,1)S(1)}, u32[]{:S(2)}, u32[]{:S(2)}) collective-permute-start(bf16[8,120,1152]{2,1,0:T(8,128)(2,1)} %copy-done.8), channel_id=1, source_target_pairs={{0,1},{1,0},{2,3},{3,2},{4,5},{5,4},{6,7},{7,6},{8,9},{9,8},{10,11... | collective-permute-start | bytes 6635528 | tf_op jit(solution)/shard_map/ppermute | solution.py:394
  41.6 27.3 %collective-permute-start = (bf16[2,120,4608]{2,1,0:T(8,128)(2,1)}, bf16[2,120,4608]{2,1,0:T(8,128)(2,1)}, u32[]{:S(2)}, u32[]{:S(2)}) collective-permute-start(bf16[2,120,4608]{2,1,0:T(8,128)(2,1)} %param.8), channel_id=1, source_target_pairs={{0,1},{1,0},{2,3},{3,2},{4,5},{5,4},{6,7},{7,6},{8,9},{9,8},{10,11... | collective-permute-start | bytes 6635528 | tf_op jit(solution)/shard_map/ppermute | solution.py:394
  50.3 4.6 %copy-start.12 = (bf16[480,480]{1,0:T(8,128)(2,1)S(1)}, bf16[480,480]{1,0:T(8,128)(2,1)}, u32[]{:S(2)}) copy-start(bf16[480,480]{1,0:T(8,128)(2,1)} %param.10) | copy-start | bytes 1382404
  50.3 5.1 %copy-start.13 = (bf16[96,96]{1,0:T(8,128)(2,1)S(1)}, bf16[96,96]{1,0:T(8,128)(2,1)}, u32[]{:S(2)}) copy-start(bf16[96,96]{1,0:T(8,128)(2,1)} %param.9) | copy-start | bytes 55300
  50.3 56.9 %all-to-all-start.1 = ((bf16[4,2,120,1152]{3,2,1,0:T(8,128)(2,1)}), bf16[4,2,120,1152]{3,2,1,0:T(8,128)(2,1)}, u32[]{:S(2)}, u32[]{:S(2)}) async-start(bf16[4,2,120,1152]{3,2,1,0:T(8,128)(2,1)} %bitcast.45), calls=%async_computation.1 | async-start | bytes 4423680 | tf_op jit(solution)/shard_map/all_to_all | solution.py:397
  64.6 4.2 %copy-start.6 = (bf16[384,384]{1,0:T(8,128)(2,1)}, bf16[384,384]{1,0:T(8,128)(2,1)S(1)}, u32[]{:S(2)}) copy-start(bf16[384,384]{1,0:T(8,128)(2,1)S(1)} %mul.104.refs_5_) | copy-start | bytes 884740
  64.9 4.0 %copy-start.2 = (f32[12,4,4608]{2,1,0:T(4,128)S(1)}, f32[12,4,4608]{2,1,0:T(4,128)}, u32[]{:S(2)}) copy-start(f32[12,4,4608]{2,1,0:T(4,128)} %reshape_reshape.12.refs_2_) | copy-start | bytes 2654212
  64.9 4.0 %copy-start.3 = (f32[12,4,4608]{2,1,0:T(4,128)S(1)}, f32[12,4,4608]{2,1,0:T(4,128)}, u32[]{:S(2)}) copy-start(f32[12,4,4608]{2,1,0:T(4,128)} %reshape_reshape.13.refs_3_) | copy-start | bytes 2654212
  105.7 1.4 copy-start
  107.1 4.3 %copy-start.16 = (s32[8]{0:T(128)S(1)}, s32[8]{0:T(128)}, u32[]{:S(2)}) copy-start(s32[8]{0:T(128)} %param.13) | copy-start | bytes 100
  107.1 4.4 %copy-start.14 = (bf16[96,96]{1,0:T(8,128)(2,1)S(1)}, bf16[96,96]{1,0:T(8,128)(2,1)}, u32[]{:S(2)}) copy-start(bf16[96,96]{1,0:T(8,128)(2,1)} %param.9) | copy-start | bytes 55300
  107.1 30.7 %all-to-all-start.2 = ((bf16[4,2,120,1152]{3,2,1,0:T(8,128)(2,1)}), bf16[4,2,120,1152]{3,2,1,0:T(8,128)(2,1)S(1)}, u32[]{:S(2)}, u32[]{:S(2)}) async-start(bf16[4,2,120,1152]{3,2,1,0:T(8,128)(2,1)} %shard_map.95), calls=%async_computation.2 | async-start | bytes 4423680 | tf_op jit(solution)/shard_map/all_to_all | solution.py:397
  111.5 1.6 copy-start.10
  111.5 1.6 copy-start.11
  117.8 77.9 %collective-permute-start.2 = (bf16[2,2,120,1152]{3,2,1,0:T(8,128)(2,1)}, bf16[2,2,120,1152]{3,2,1,0:T(8,128)(2,1)}, u32[]{:S(2)}, u32[]{:S(2)}) collective-permute-start(bf16[2,2,120,1152]{3,2,1,0:T(8,128)(2,1)} %get-tuple-element.41), channel_id=1, source_target_pairs={{0,1},{1,0},{2,3},{3,2},{4,5},{5,4},{6,7},{7,6},{8,9},{9,8},{10,11... | collective-permute-start | bytes 3317768 | tf_op jit(solution)/shard_map/ppermute | solution.py:394
  137.9 1.4 copy-start.9
  139.2 66.5 %all-to-all-start.3 = ((bf16[4,2,120,1152]{3,2,1,0:T(8,128)(2,1)}), bf16[4,2,120,1152]{3,2,1,0:T(8,128)(2,1)S(1)}, u32[]{:S(2)}, u32[]{:S(2)}) async-start(bf16[4,2,120,1152]{3,2,1,0:T(8,128)(2,1)} %pad_maximum_fusion.2), calls=%async_computation.3 | async-start | bytes 4423680 | tf_op jit(solution)/shard_map/all_to_all | solution.py:397
  152.7 1.2 copy-start.4
  153.8 1.2 copy-start.5
  155.0 1.0 copy-start.7
  156.0 37.1 %copy-start.1 = (f32[240,2304]{1,0:T(8,128)S(1)}, f32[240,2304]{1,0:T(8,128)}, u32[]{:S(2)}) copy-start(f32[240,2304]{1,0:T(8,128)} %copy-done) | copy-start | bytes 6635524
  201.1 2.7 collective-permute-start.4
  205.7 56.1 %all-to-all-start.4 = ((bf16[4,2,120,1152]{3,2,1,0:T(8,128)(2,1)}), bf16[4,2,120,1152]{3,2,1,0:T(8,128)(2,1)}, u32[]{:S(2)}, u32[]{:S(2)}) async-start(bf16[4,2,120,1152]{3,2,1,0:T(8,128)(2,1)} %pad_maximum_fusion.3), calls=%async_computation.4 | async-start | bytes 4423680 | tf_op jit(solution)/shard_map/all_to_all | solution.py:397
  210.8 4.3 %collective-permute-start.3 = (bf16[8,120,1152]{2,1,0:T(8,128)(2,1)S(1)}, bf16[8,120,1152]{2,1,0:T(8,128)(2,1)S(1)}, u32[]{:S(2)}, u32[]{:S(2)}) collective-permute-start(bf16[8,120,1152]{2,1,0:T(8,128)(2,1)S(1)} %bitcast.40), channel_id=1, source_target_pairs={{0,1},{1,0},{2,3},{3,2},{4,5},{5,4},{6,7},{7,6},{8,9},{9,8},{10,11... | collective-permute-start | bytes 6635528 | tf_op jit(solution)/shard_map/ppermute | solution.py:394
